TPU v7x, 256 devices: a whole 4x4x8 slice. The times are simulated.
256 devices in a mesh: row: 16 (over y, z_hi, core), col: 16 (over z_lo, x).
Axes of the slice: x: 4, y: 4, z: 8 (z_hi: 2, z_lo: 4; z = z_hi * 4 + z_lo), core: 2. Of those that a mesh axis runs over, the one named last changes fastest.
Arguments:
- fluid_data: float32 [51, 32768], P(None, ('row', 'col')), as said below
- center_data: float32 [51, 16384], P(None, ('col', 'row')), as said below
- poly_coef: float32 [48, 4], replicated, may hold values from -3 to 3
Outputs:
- fluid_motion: float32 [48, 32768], P(None, ('row', 'col'))
- center_load: float32 [48, 16384], P(None, ('col', 'row'))
Inputs may be any that keep to these rules, and one draw needn't show every extreme that they name: Rows 0 to 2 of fluid_data lie in [0, 1]; rows 3 and on are forces. Rows 0 and 1 of center_data lie in [0, 1] and row 2 lies in [-0.5, -0.02], so every center is at least 0.02 below every vertex; rows 3 and on are coefficients.
All inputs are finite; a program needn't handle non-finite values.
Results may differ from a plain program's by a relative error of at most 0.0003.
Values sent between devices are 32-bit elements; how exact they have to be, the bound alone decides.
A program may use at most 64 MiB of HBM per device.

v0:
```python
import math

import jax
import jax.numpy as jnp
from jax import lax
from jax.sharding import PartitionSpec as P

WAVES = 64


def from_everyone(array, axis):
    devices = lax.axis_size(axis)
    return lax.all_to_all(
        jnp.broadcast_to(array[None], (devices, *array.shape)), axis, 0, 0, tiled=True
    )


def in_order(parts, dim):
    parts = jnp.moveaxis(parts, 0, dim)
    shape = parts.shape
    return parts.reshape(*shape[:dim], shape[dim] * shape[dim + 1], *shape[dim + 2 :])


def gather_directly(array, axis, dim):
    parts = from_everyone(array, axis)
    return in_order(parts, dim)


def split_up(array, dim, devices):
    before, after = (array.shape[:dim], array.shape[dim + 1 :])
    return jnp.moveaxis(array.reshape(*before, devices, -1, *after), dim, 0)


def sum_at_owner(array, axis, dim):
    parts = split_up(array, dim, lax.axis_size(axis))
    arrived = lax.all_to_all(parts, axis, split_axis=0, concat_axis=0, tiled=True)
    return arrived.sum(axis=0)


def kernel_block(center_pos, fluid_pos):
    dx = center_pos[0][:, None] - fluid_pos[0][None, :]
    dy = center_pos[1][:, None] - fluid_pos[1][None, :]
    dz = center_pos[2][:, None] - fluid_pos[2][None, :]
    sq = dx * dx + dy * dy + dz * dz
    phase = 2.0 * math.pi * WAVES * jnp.sqrt(sq)
    return jnp.sin(phase) / phase


def both_maps(centers, fluid):
    total = centers.shape[1]
    width = fluid.shape[1]
    block = math.gcd(total, max(128, 2**20 // width))
    count = total // block
    fluid_pos = fluid[:3]
    forces = fluid[3:]
    pieces = centers.reshape(centers.shape[0], count, block).transpose(1, 0, 2)

    def step(motion, piece):
        tile = kernel_block(piece[:3], fluid_pos)
        motion = motion + jnp.dot(
            piece[3:], tile, precision=lax.Precision.HIGHEST, preferred_element_type=jnp.float32
        )
        back = lax.dot_general(
            forces,
            tile,
            (((1,), (1,)), ((), ())),
            precision=lax.Precision.HIGHEST,
            preferred_element_type=jnp.float32,
        )
        return (motion, back)

    start = jnp.zeros((forces.shape[0], width), jnp.float32)
    motion, backs = lax.scan(step, start, pieces)
    loads = backs.transpose(1, 0, 2).reshape(forces.shape[0], total)
    return (motion, loads)


def per_device(fluid_data, center_data, poly_coef):
    fluid_block = gather_directly(fluid_data, "col", 1)
    center_block = gather_directly(center_data, "row", 1)
    partial_motion, partial_loads = both_maps(center_block, fluid_block)
    motion = sum_at_owner(partial_motion, "col", 1)
    loads = sum_at_owner(partial_loads, "row", 1)
    affine = poly_coef[:, 0:1] + jnp.dot(
        poly_coef[:, 1:],
        fluid_data[:3],
        precision=lax.Precision.HIGHEST,
        preferred_element_type=jnp.float32,
    )
    return (motion + affine, loads)


def solution(mesh):
    placed = (P(None, ("row", "col")), P(None, ("col", "row")), P())
    return jax.shard_map(
        per_device,
        mesh=mesh,
        in_specs=placed,
        out_specs=(P(None, ("row", "col")), P(None, ("col", "row"))),
        check_vma=False,
    )
```

profile of v0, /device:TPU:1, one launch (start us, length us, event | category | flops | bytes accessed | tf_op | source)
XLA Modules:
  0.0 172.9 jit_solution(15485215940686679854)
XLA Ops:
  0.6 0.8 broadcast_in_dim.24
  1.4 0.3 reshape.24
  1.7 23.2 %all_to_all.20 = f32[16,1,3264]{2,1,0:T(1,128)S(1)} all-to-all(f32[16,1,3264]{2,1,0:T(1,128)S(1)} %reshape.24), channel_id=1, replica_groups=mesh['row'=16,'col'=16] {'row'}, dimensions={0} | all-to-all | bytes 417792 | tf_op jit(solution)/shard_map/all_to_all | solution.py:13
  24.9 0.8 broadcast_in_dim.25
  25.7 7.2 %all-to-all-start.1 = ((f32[16,51,128]{2,1,0:T(8,128)}), f32[16,51,128]{2,1,0:T(8,128)S(1)}, u32[]{:S(2)}, u32[]{:S(2)}) async-start(f32[16,51,128]{2,1,0:T(8,128)} %broadcast_in_dim.25), calls=%async_computation.1 | async-start | bytes 917504 | tf_op jit(solution)/shard_map/all_to_all | solution.py:13
  33.0 0.5 broadcast.19
  33.5 1.1 reduce
  34.6 0.1 reshape.25
  34.8 0.1 copy.11
  34.9 0.2 reshape_reshape.6
  35.0 10.6 %all-to-all-done.1 = f32[16,51,128]{2,1,0:T(8,128)S(1)} async-done(((f32[16,51,128]{2,1,0:T(8,128)}), f32[16,51,128]{2,1,0:T(8,128)S(1)}, u32[]{:S(2)}, u32[]{:S(2)}) %all-to-all-start.1) | async-done | bytes 417824 | tf_op jit(solution)/shard_map/all_to_all | solution.py:13
  45.7 91.1 %while.13 = (s32[]{:T(128)}, f32[48,2048]{1,0:T(8,128)S(1)}, f32[2,48,512]{2,1,0:T(8,128)S(1)}, f32[2,51,512]{2,0,1:T(2,128)S(1)}, f32[3,2048]{1,0:T(4,128)S(1)}...) while((s32[]{:T(128)}, f32[48,2048]{1,0:T(8,128)S(1)}, ...), condition=%wide.region_1.2_spmd.clone, body=%wide.region_0.1_spmd.clone.sunk | while | flops 1229127680 | bytes 1695923 | solution.py:73
  45.9 0.1 constant_dynamic-slice_fusion.7
  46.1 19.3 %convolution_add_fusion.3 = f32[48,2048]{1,0:T(8,128)S(1)} fusion(f32[2048]{0:T(1024)S(1)} %bitcast.67, f32[512]{0:T(512)S(1)} %bitcast.76, f32[2048]{0:T(1024)S(1)} %bitcast.69, f32[512]{0:T(512)S(1)} %bitcast.74, f32[2048]{0:T(1024)S(1)} %bitcast.65, f32[512]{0:T(512)S(1)} %bitcast.72, f32[48,2048]{1,0:T(8,128)S(1)} %get-tuple-element.155, ...), kind=kOutput, calls=%fused_computation.1.clone.1 | convolution fusion | flops 614662144 | bytes 915457 | tf_op jit(solution)/shard_map/while/body/eval_jaxpr/dot_general | solution.py:60
  65.4 20.2 %fusion.15 = f32[2,48,512]{2,1,0:T(8,128)S(1)} fusion(f32[2,48,512]{2,1,0:T(8,128)S(1)} %get-tuple-element.156, s32[]{:T(128)} %get-tuple-element.154, f32[48,2048]{1,0:T(8,128)S(1)} %get-tuple-element.170, f32[2048]{0:T(1024)S(1)} %bitcast.68, f32[512]{0:T(512)S(1)} %bitcast.77, f32[2048]{0:T(1024)S(1)} %bitcast.70, f32[512]{0:T(512)S(1)} %bitcast.75, ...), kind=kOutput, calls=%fused_computation.4.clone.1 | convolution fusion | flops 614465536 | bytes 522244 | tf_op jit(solution)/shard_map/while/body/eval_jaxpr/dot_general | solution.py:63
  90.4 0.1 constant_dynamic-slice_fusion.7
  90.5 19.0 %convolution_add_fusion.3 = f32[48,2048]{1,0:T(8,128)S(1)} fusion(f32[2048]{0:T(1024)S(1)} %bitcast.67, f32[512]{0:T(512)S(1)} %bitcast.76, f32[2048]{0:T(1024)S(1)} %bitcast.69, f32[512]{0:T(512)S(1)} %bitcast.74, f32[2048]{0:T(1024)S(1)} %bitcast.65, f32[512]{0:T(512)S(1)} %bitcast.72, f32[48,2048]{1,0:T(8,128)S(1)} %get-tuple-element.155, ...), kind=kOutput, calls=%fused_computation.1.clone.1 | convolution fusion | flops 614662144 | bytes 915457 | tf_op jit(solution)/shard_map/while/body/eval_jaxpr/dot_general | solution.py:60
  109.5 20.5 %fusion.15 = f32[2,48,512]{2,1,0:T(8,128)S(1)} fusion(f32[2,48,512]{2,1,0:T(8,128)S(1)} %get-tuple-element.156, s32[]{:T(128)} %get-tuple-element.154, f32[48,2048]{1,0:T(8,128)S(1)} %get-tuple-element.170, f32[2048]{0:T(1024)S(1)} %bitcast.68, f32[512]{0:T(512)S(1)} %bitcast.77, f32[2048]{0:T(1024)S(1)} %bitcast.70, f32[512]{0:T(512)S(1)} %bitcast.75, ...), kind=kOutput, calls=%fused_computation.4.clone.1 | convolution fusion | flops 614465536 | bytes 522244 | tf_op jit(solution)/shard_map/while/body/eval_jaxpr/dot_general | solution.py:63
  136.8 0.2 copy.15
  136.9 0.3 reshape_reshape.7
  137.2 0.1 copy.16
  137.3 0.9 reshape.26
  138.2 5.9 %all-to-all-start.3 = ((f32[16,1,3072]{2,1,0:T(1,128)}), f32[16,1,3072]{2,1,0:T(1,128)S(1)}, u32[]{:S(2)}, u32[]{:S(2)}) async-start(f32[16,1,3072]{2,1,0:T(1,128)} %reshape.26), calls=%async_computation.3 | async-start | bytes 393216 | tf_op jit(solution)/shard_map/all_to_all | solution.py:36
  144.1 0.1 copy.23
  144.2 0.9 copy.14
  145.0 9.8 %all-to-all-done.3 = f32[16,1,3072]{2,1,0:T(1,128)S(1)} async-done(((f32[16,1,3072]{2,1,0:T(1,128)}), f32[16,1,3072]{2,1,0:T(1,128)S(1)}, u32[]{:S(2)}, u32[]{:S(2)}) %all-to-all-start.3) | async-done | bytes 196640 | tf_op jit(solution)/shard_map/all_to_all | solution.py:36
  154.8 5.4 %all-to-all-start.2 = ((f32[16,48,128]{2,1,0:T(8,128)}), f32[16,48,128]{2,1,0:T(8,128)S(1)}, u32[]{:S(2)}, u32[]{:S(2)}) async-start(f32[16,48,128]{2,1,0:T(8,128)} %copy.14), calls=%async_computation.2 | async-start | bytes 786432 | tf_op jit(solution)/shard_map/all_to_all | solution.py:36
  160.2 1.1 reduce.1
  161.3 0.1 reshape.27
  161.4 0.6 reduce_sum.19
  162.1 9.7 %all-to-all-done.2 = f32[16,48,128]{2,1,0:T(8,128)S(1)} async-done(((f32[16,48,128]{2,1,0:T(8,128)}), f32[16,48,128]{2,1,0:T(8,128)S(1)}, u32[]{:S(2)}, u32[]{:S(2)}) %all-to-all-start.2) | async-done | bytes 393248 | tf_op jit(solution)/shard_map/all_to_all | solution.py:36
  171.8 0.8 fusion.5
  (14 shorter events, 0.1 us)
Async XLA Ops:
  1.4 23.5 %copy-start = (f32[51,128]{1,0:T(8,128)S(1)}, f32[51,128]{1,0:T(8,128)}, u32[]{:S(2)}) copy-start(f32[51,128]{1,0:T(8,128)} %param.5) | copy-start | bytes 78340
  25.7 19.9 %all-to-all-start.1 = ((f32[16,51,128]{2,1,0:T(8,128)}), f32[16,51,128]{2,1,0:T(8,128)S(1)}, u32[]{:S(2)}, u32[]{:S(2)}) async-start(f32[16,51,128]{2,1,0:T(8,128)} %broadcast_in_dim.25), calls=%async_computation.1 | async-start | bytes 917504 | tf_op jit(solution)/shard_map/all_to_all | solution.py:13
  138.2 16.6 %all-to-all-start.3 = ((f32[16,1,3072]{2,1,0:T(1,128)}), f32[16,1,3072]{2,1,0:T(1,128)S(1)}, u32[]{:S(2)}, u32[]{:S(2)}) async-start(f32[16,1,3072]{2,1,0:T(1,128)} %reshape.26), calls=%async_computation.3 | async-start | bytes 393216 | tf_op jit(solution)/shard_map/all_to_all | solution.py:36
  145.0 15.1 %copy-start.1 = (f32[48,4]{0,1:T(4,128)S(1)}, f32[48,4]{0,1:T(4,128)}, u32[]{:S(2)}) copy-start(f32[48,4]{0,1:T(4,128)} %param.7) | copy-start | bytes 2308
  154.8 17.0 %all-to-all-start.2 = ((f32[16,48,128]{2,1,0:T(8,128)}), f32[16,48,128]{2,1,0:T(8,128)S(1)}, u32[]{:S(2)}, u32[]{:S(2)}) async-start(f32[16,48,128]{2,1,0:T(8,128)} %copy.14), calls=%async_computation.2 | async-start | bytes 786432 | tf_op jit(solution)/shard_map/all_to_all | solution.py:36
where the time goes:
time: 175 us; the launch traced here: 173 us
  matrix products  79.9 us (46%)
  waiting for transfers between devices  30 us (17%)
  blocking collectives  23.2 us (13%)
  starting transfers between devices  18.5 us (11%)
  loops' own time  11.8 us (7%)
  local copies, waits for them, and re-layouts  5.59 us (3%)
  other arithmetic  2.93 us (2%)
    dot_general x2, matrix products, step(): lax.dot_general(forces, tile, (((1,), (1,)), ((), ())), precision=lax.Pre...  40.7 us
    dot_general x2, matrix products, step(): jnp.dot(piece[3:], tile, precision=lax.Precision.HIGHEST, preferred_eleme...  38.3 us
    all_to_all x1, blocking collectives, from_everyone(): lax.all_to_all(jnp.broadcast_to(array[None], (devices, *array.shape)), ax...  23.2 us
    all_to_all x2, waiting for transfers between devices, sum_at_owner(): lax.all_to_all(parts, axis, split_axis=0, concat_axis=0, tiled=True)  19.5 us
    another operation x1, loops' own time, both_maps(): motion, backs = lax.scan(step, start, pieces)  11.8 us
    all_to_all x2, starting transfers between devices, sum_at_owner(): lax.all_to_all(parts, axis, split_axis=0, concat_axis=0, tiled=True)  11.2 us
    all_to_all x1, waiting for transfers between devices, from_everyone(): lax.all_to_all(jnp.broadcast_to(array[None], (devices, *array.shape)), ax...  10.6 us
    all_to_all x1, starting transfers between devices, from_everyone(): lax.all_to_all(jnp.broadcast_to(array[None], (devices, *array.shape)), ax...  7.22 us
  transfers between devices with their start and end apart: 3, of which 3 were waited for; matrix products, arithmetic and copies ran while one was open for 3% of the time, Pallas kernels for 0%

commit v1 on v0

v1 whole, which is shorter than its diff:
```python
import jax
import jax.numpy as jnp
from jax import lax
from jax.experimental import pallas as pl
from jax.experimental.pallas import tpu as pltpu
from jax.sharding import PartitionSpec as P

WAVES = 64
COLS = 48
PLANE = [
    (0, 0), (1, 0), (3, 0), (0, 1), (0, 3), (2, 0), (0, 2), (1, 1),
    (1, 3), (3, 1), (3, 3), (2, 1), (2, 3), (1, 2), (3, 2), (2, 2),
]
LINE = [
    (0, 0), (0, 1), (1, 0), (1, 1), (7, 0), (7, 1), (2, 0), (2, 1),
    (6, 0), (6, 1), (3, 0), (3, 1), (5, 0), (5, 1), (4, 0), (4, 1),
]
HALF = 512
TILES = 8
STRIP = 32
S = (0.9999999765898422, -6.57972875383963, 12.987203158835507, -12.183276227896942, 6.292462070004323)
F32 = jnp.float32
BF16 = jnp.bfloat16


def split(value):
    high = value.astype(BF16)
    return high, (value - high.astype(F32)).astype(BF16)


def body(
    fluid_ref, center_ref, poly_ref, motion_ref, load_ref,
    fbuf, cbuf, cb, fpos, fhl, chl, kh0, kl0, kh1, kl1, lacc, macc, mrecv, lsend, lrecv,
    fs, fr, cs, cr, ms, mr, ls, lr,
):
    row, col = lax.axis_index("row"), lax.axis_index("col")
    core, z_hi, y = row % 2, (row // 2) % 2, row // 4
    x, z_lo = col % 4, col // 4
    z = z_hi * 4 + z_lo

    def plane_dev(k):
        dx, dy = PLANE[k]
        return {"row": (row + 4 * dy) % 16, "col": z_lo * 4 + (x + dx) % 4}

    def line_dev(k):
        dz, dc = LINE[k]
        z2 = (z + dz) % 8
        return {"row": 4 * y + 2 * (z2 // 4) + (core + dc) % 2, "col": (z2 % 4) * 4 + x}

    def back_plane_dev(k):
        dx, dy = PLANE[k]
        return {"row": (row + 4 * (4 - dy)) % 16, "col": z_lo * 4 + (x + 4 - dx) % 4}

    def back_line_dev(k):
        dz, dc = LINE[k]
        z2 = (z + 8 - dz) % 8
        return {"row": 4 * y + 2 * (z2 // 4) + (core + dc) % 2, "col": (z2 % 4) * 4 + x}

    def remote(src, dst, send, recv, dev):
        return pltpu.make_async_remote_copy(
            src_ref=src, dst_ref=dst, send_sem=send, recv_sem=recv,
            device_id=dev, device_id_type=pl.DeviceIdType.MESH,
        )

    barrier = pltpu.get_barrier_semaphore()
    for k in range(1, 16):
        for dev in (plane_dev(k), line_dev(k)):
            pl.semaphore_signal(barrier, inc=1, device_id=dev, device_id_type=pl.DeviceIdType.MESH)

    fbuf[0, 0:COLS, :] = fluid_ref[3:51, :]
    fbuf[0, COLS:56, :] = jnp.zeros((8, 128), F32)
    fbuf[0, COLS:51, :] = fluid_ref[0:3, :] * WAVES
    cbuf[0, 0:24, 0:64] = center_ref[3:27, :]
    cbuf[0, 0:24, 64:128] = center_ref[27:51, :]
    cbuf[0, 24:32, :] = jnp.zeros((8, 128), F32)
    cbuf[0, 24:27, 0:64] = center_ref[0:3, :] * WAVES
    fhl[:, 96:128, :] = jnp.zeros((TILES, 32, 256), BF16)

    pl.semaphore_wait(barrier, 30)
    fcopy = [None] + [
        remote(fbuf.at[0], fbuf.at[k], fs.at[k], fr.at[k], plane_dev(k)) for k in range(1, 16)
    ]
    ccopy = [None] + [
        remote(cbuf.at[0], cbuf.at[k], cs.at[k], cr.at[k], line_dev(k)) for k in range(1, 16)
    ]
    for k in range(1, 16):
        ccopy[k].start()
        fcopy[k].start()

    low = lax.broadcasted_iota(jnp.int32, (24, 128), 1) < 64

    def turn(value):
        return pltpu.roll(value, 64, 1)

    def unpack_centers(m):
        a, b = cbuf[2 * m], cbuf[2 * m + 1]
        lanes = pl.ds(m * 128, 128)
        coef = jnp.concatenate(
            [jnp.where(low, a[0:24], turn(b[0:24])), jnp.where(low, turn(a[0:24]), b[0:24])], axis=0
        )
        high, rest = split(coef)
        chl[0:COLS, lanes] = high
        chl[COLS:96, lanes] = rest
        places = jnp.where(low[0:8], a[24:32], turn(b[24:32]))
        for axis in range(3):
            line = jnp.broadcast_to(places[axis : axis + 1], (128, 128))
            cb[axis, m * 128 : (m + 1) * 128, :] = line.T

    def unpack_fluid(n):
        for part in range(2):
            high, rest = split(fbuf[2 * n + part, 0:COLS, :])
            lanes = pl.ds(part * 128, 128)
            fhl[n, 0:COLS, lanes] = high
            fhl[n, COLS:96, lanes] = rest

    def kernel_tile(half, n, kh, kl):
        places = [[fbuf[2 * n + part, COLS + axis : COLS + axis + 1, :] for axis in range(3)] for part in range(2)]
        for first in range(0, HALF, STRIP):
            rows = pl.ds(half * HALF + first, STRIP)
            at = [cb[axis, rows, :] for axis in range(3)]
            for part in range(2):
                dx, dy, dz = (at[axis] - places[part][axis] for axis in range(3))
                sq = dx * dx + dy * dy + dz * dz
                inverse = lax.rsqrt(sq)
                turns = sq * inverse - 0.25
                b = 0.25 - jnp.abs(turns - jnp.round(turns))
                b2 = b * b
                value = S[4]
                for coefficient in (S[3], S[2], S[1], S[0]):
                    value = value * b2 + coefficient
                high, rest = split(value * (b * inverse))
                kh[first : first + STRIP, part * 128 : (part + 1) * 128] = high
                kl[first : first + STRIP, part * 128 : (part + 1) * 128] = rest

    def products(half, n, kh, kl):
        coef = chl[:, half * HALF : (half + 1) * HALF]
        high, rest = kh[...], kl[...]
        motion = jnp.dot(coef, high, preferred_element_type=F32) + jnp.dot(
            coef, rest, preferred_element_type=F32
        )
        motion = motion[0:COLS] + motion[COLS:96]
        for part in range(2):
            piece = motion[:, part * 128 : (part + 1) * 128]
            if half == 0:
                macc[2 * n + part] = piece
            else:
                macc[2 * n + part] += piece
        forces = fhl[n]
        across = (((1,), (1,)), ((), ()))
        load = lax.dot_general(high, forces, across, preferred_element_type=F32) + lax.dot_general(
            rest, forces, across, preferred_element_type=F32
        )
        if n == (0 if half == 0 else TILES - 1):
            lacc[half] = load
        else:
            lacc[half] += load

    def send_loads(half):
        total = lacc[half]
        total = (total + pltpu.roll(total, 80, 1)).T[0:COLS]
        copies = []
        for pair in range(4):
            m = half * 4 + pair
            piece = total[:, pair * 128 : (pair + 1) * 128]
            top, bottom = piece[0:24], piece[24:48]
            lsend[2 * m] = jnp.where(low, top, turn(bottom))
            lsend[2 * m + 1] = jnp.where(low, turn(top), bottom)
            for k in (2 * m, 2 * m + 1):
                if k > 0:
                    copy = remote(lsend.at[k], lrecv.at[k], ls.at[k], lr.at[k], back_line_dev(k))
                    copy.start()
                    copies.append(copy)
        return copies

    def send_motion(n):
        copies = []
        for k in (2 * n, 2 * n + 1):
            if k > 0:
                copy = remote(macc.at[k], mrecv.at[k], ms.at[k], mr.at[k], back_plane_dev(k))
                copy.start()
                copies.append(copy)
        return copies

    buffers = ((kh0, kl0), (kh1, kl1))
    order = [(0, n) for n in range(TILES)] + [(1, n) for n in reversed(range(TILES))]
    sent = []
    for m in range(4):
        for k in (2 * m, 2 * m + 1):
            if k > 0:
                ccopy[k].wait_recv()
        unpack_centers(m)
    for step, (half, n) in enumerate(order):
        if half == 0:
            for k in (2 * n, 2 * n + 1):
                if k > 0:
                    fcopy[k].wait_recv()
            unpack_fluid(n)
        if half == 1 and n == TILES - 1:
            for m in range(4, 8):
                for k in (2 * m, 2 * m + 1):
                    ccopy[k].wait_recv()
                unpack_centers(m)
        kernel_tile(half, n, *buffers[step % 2])
        if step > 0:
            products(*order[step - 1], *buffers[(step - 1) % 2])
        if step > 1 and order[step - 2][0] == 1:
            sent += send_motion(order[step - 2][1])
        if step > 1 and order[step - 2] == (0, TILES - 1):
            sent += send_loads(0)
    products(*order[-1], *buffers[(len(order) - 1) % 2])
    sent += send_motion(order[-2][1])
    sent += send_loads(1)
    sent += send_motion(order[-1][1])

    motion = macc[0] + poly_ref[:, 0:1]
    for axis in range(3):
        motion += poly_ref[:, axis + 1 : axis + 2] * fluid_ref[axis : axis + 1, :]
    for copy in sent:
        copy.wait_recv()
    for k in range(1, 16):
        motion += mrecv[k]
    motion_ref[...] = motion
    load = lsend[0]
    for k in range(1, 16):
        load += lrecv[k]
    load_ref[0:24, :] = load[:, 0:64]
    load_ref[24:48, :] = load[:, 64:128]

    for copy in sent:
        copy.wait_send()
    for k in range(1, 16):
        fcopy[k].wait_send()
        ccopy[k].wait_send()


def per_device(fluid_data, center_data, poly_coef):
    vmem = pl.BlockSpec(memory_space=pltpu.VMEM)
    dma = pltpu.SemaphoreType.DMA((16,))
    return pl.pallas_call(
        body,
        out_shape=(
            jax.ShapeDtypeStruct((COLS, 128), F32),
            jax.ShapeDtypeStruct((COLS, 64), F32),
        ),
        in_specs=[vmem] * 3,
        out_specs=(vmem, vmem),
        scratch_shapes=[
            pltpu.VMEM((16, 56, 128), F32),
            pltpu.VMEM((16, 32, 128), F32),
            pltpu.VMEM((3, 1024, 128), F32),
            pltpu.VMEM((8, 128), F32),
            pltpu.VMEM((TILES, 128, 256), BF16),
            pltpu.VMEM((96, 1024), BF16),
            pltpu.VMEM((HALF, 256), BF16),
            pltpu.VMEM((HALF, 256), BF16),
            pltpu.VMEM((HALF, 256), BF16),
            pltpu.VMEM((HALF, 256), BF16),
            pltpu.VMEM((2, HALF, 128), F32),
            pltpu.VMEM((16, COLS, 128), F32),
            pltpu.VMEM((16, COLS, 128), F32),
            pltpu.VMEM((16, 24, 128), F32),
            pltpu.VMEM((16, 24, 128), F32),
            *([dma] * 8),
        ],
        compiler_params=pltpu.CompilerParams(collective_id=0, has_side_effects=True),
        name="couple",
    )(fluid_data, center_data, poly_coef)


def solution(mesh):
    return jax.shard_map(
        per_device,
        mesh=mesh,
        in_specs=(P(None, ("row", "col")), P(None, ("col", "row")), P()),
        out_specs=(P(None, ("row", "col")), P(None, ("col", "row"))),
        check_vma=False,
    )
```

time: 175 us -> 43.8 us (0.25); the launches traced: 173 us -> 43.5 us
  matrix products: 79.9 us -> 0 us
  Pallas kernels: 0 us -> 39.5 us
  waiting for transfers between devices: 30 us -> 0 us
  blocking collectives: 23.2 us -> 0 us
  starting transfers between devices: 18.5 us -> 0 us
  loops' own time: 11.8 us -> 0 us
  other arithmetic: 2.93 us -> 0 us
  local copies, waits for them, and re-layouts: 5.59 us -> 3.34 us
    dot_general x5 -> x0, matrix products: 79.9 us -> none  [the longest x2 40.7 us: step(): lax.dot_general(forces, tile, (((1,), (1,)), ((), ())), precision=lax.Pre...]
    pallas_call x0 -> x1, Pallas kernels: none -> 39.5 us  [per_device(): pl.pallas_call(body, out_shape=(jax.ShapeDtypeStruct((COLS, 128), F32), j...]
    all_to_all x3 -> x0, waiting for transfers between devices: 30 us -> none  [the longest x2 19.5 us: sum_at_owner(): lax.all_to_all(parts, axis, split_axis=0, concat_axis=0, tiled=True)]
    all_to_all x1 -> x0, blocking collectives: 23.2 us -> none  [from_everyone(): lax.all_to_all(jnp.broadcast_to(array[None], (devices, *array.shape)), ax...]
    all_to_all x3 -> x0, starting transfers between devices: 18.5 us -> none  [the longest x2 11.2 us: sum_at_owner(): lax.all_to_all(parts, axis, split_axis=0, concat_axis=0, tiled=True)]
    another operation x1 -> x0, loops' own time: 11.8 us -> none  [both_maps(): motion, backs = lax.scan(step, start, pieces)]
    all_to_all x2 -> x0, other arithmetic: 2.25 us -> none  [the longest x1 1.14 us: from_everyone(): lax.all_to_all(jnp.broadcast_to(array[None], (devices, *array.shape)), ax...]
    unnamed x9 -> x5, local copies, waits for them, and re-layouts: 1.54 us -> 3.34 us
  transfers between devices with their start and end apart: 3 -> 0, of which waited for: 3 -> 0; matrix products, arithmetic and copies ran while one was open for 3% -> 0% of each run, Pallas kernels for 0% -> 0%
where the time goes in v1:
time: 43.8 us; the launch traced here: 43.5 us
  Pallas kernels  39.5 us (90%)
  local copies, waits for them, and re-layouts  3.34 us (8%)
  between operations  0.65 us (1%)
    pallas_call x1, Pallas kernels, per_device(): pl.pallas_call(body, out_shape=(jax.ShapeDtypeStruct((COLS, 128), F32), j...  39.5 us
    unnamed x5, local copies, waits for them, and re-layouts  3.34 us

profile of v1, /device:TPU:1, one launch (start us, length us, event | category | flops | bytes accessed | tf_op | source)
XLA Modules:
  0.0 43.5 jit_solution(10667074719920602930)
XLA Ops:
  0.6 1.4 %copy.5.poly_ref = f32[48,4]{1,0:T(8,128)} copy(f32[48,4]{0,1:T(4,128)} %param.5) | data formatting | bytes 1536 | tf_op args[2]
  2.0 39.5 %couple.1 = (f32[48,128]{1,0:T(8,128)}, f32[48,64]{1,0:T(8,128)}) custom-call(f32[51,128]{1,0:T(8,128)} %fluid_ref.1, f32[51,64]{1,0:T(8,128)} %center_ref.1, f32[48,4]{1,0:T(8,128)} %copy.5.poly_ref), custom_call_target="tpu_custom_call" | custom-call | tf_op jit(solution)/shard_map/couple/pallas_call | solution.py:239
  41.6 0.0 copy-start
  41.6 1.4 %copy.8 = f32[48,128]{1,0:T(8,128)} copy(f32[48,128]{1,0:T(8,128)} %get-tuple-element.4) | data formatting | bytes 49152
  42.9 0.0 copy-done
  42.9 0.6 %copy.9 = f32[48,64]{1,0:T(8,128)} copy(f32[48,64]{1,0:T(8,128)S(1)} %copy-done) | data formatting | bytes 24576
Async XLA Ops:
  41.6 1.4 %copy-start = (f32[48,64]{1,0:T(8,128)S(1)}, f32[48,64]{1,0:T(8,128)}, u32[]{:S(2)}) copy-start(f32[48,64]{1,0:T(8,128)} %get-tuple-element.5) | copy-start | bytes 36868

commit v2 on v1

v2 whole, which is shorter than its diff:
```python
import jax
import jax.numpy as jnp
from jax import lax
from jax.experimental import pallas as pl
from jax.experimental.pallas import tpu as pltpu
from jax.sharding import PartitionSpec as P

WAVES = 64
COLS = 48
PLANE = [
    (2, 2), (1, 2), (3, 2), (2, 1), (2, 3), (3, 3), (3, 1), (1, 3),
    (0, 0), (1, 0), (3, 0), (0, 1), (0, 3), (2, 0), (0, 2), (1, 1),
]
OWN = 8
OTHERS = [0, 1, 2, 3, 4, 5, 6, 7, 15, 14, 13, 12, 11, 10, 9]
LINE = [0, 1, 7, 2, 6, 3, 5, 4]
PAIRS = [(0, 2), (4, 6), (8, 10), (12, 14), (1, 3), (5, 7), (9, 11), (13, 15)]
FIRST = [0, 1, 2, 3, 4, 5, 6, 7]
SECOND = [7, 6, 5, 3, 4, 2, 1, 0]
HALF = 512
TILES = 8
STRIP = 32
SCALE = 6.292462070004323
S = [s / SCALE for s in (0.9999999765898422, -6.57972875383963, 12.987203158835507, -12.183276227896942)]
F32 = jnp.float32
BF16 = jnp.bfloat16


def split(value):
    high = value.astype(BF16)
    return high, (value - high.astype(F32)).astype(BF16)


def body(
    fluid_hbm, center_hbm, poly_hbm, motion_ref, load_ref,
    fluid_ref, center_ref, poly_ref, fbuf, cbuf, cb, fhl, chl, kh0, kl0, kh1, kl1, lacc, macc, msib, mout, mrecv, lsend, lrecv, own,
    ins, fs, fr, cs, cr, ss, sr, ms, mr, ls, lr,
):
    row, col = lax.axis_index("row"), lax.axis_index("col")
    core, z_hi, y = row % 2, (row // 2) % 2, row // 4
    x, z_lo = col % 4, col // 4
    z = z_hi * 4 + z_lo

    def plane_dev(dx, dy):
        return {"row": (row + 4 * dy) % 16, "col": z_lo * 4 + (x + dx) % 4}

    def line_dev(dz, flip=0):
        z2 = (z + dz) % 8
        return {"row": 4 * y + 2 * (z2 // 4) + (core + flip) % 2, "col": (z2 % 4) * 4 + x}

    def remote(src, dst, send, recv, dev):
        return pltpu.make_async_remote_copy(
            src_ref=src, dst_ref=dst, send_sem=send, recv_sem=recv,
            device_id=dev, device_id_type=pl.DeviceIdType.MESH,
        )

    fetched = [
        pltpu.make_async_copy(source, target, ins.at[i])
        for i, (source, target) in enumerate(
            ((fluid_hbm, fluid_ref), (center_hbm, center_ref), (poly_hbm, poly_ref))
        )
    ]
    for copy in fetched:
        copy.start()
    sibling = line_dev(0, 1)
    barrier = pltpu.get_barrier_semaphore()
    peers = [plane_dev(*PLANE[k]) for k in OTHERS]
    peers += [line_dev(LINE[i]) for i in range(1, 8)] + [sibling]
    for dev in peers:
        pl.semaphore_signal(barrier, inc=1, device_id=dev, device_id_type=pl.DeviceIdType.MESH)

    for copy in fetched:
        copy.wait()

    fbuf[0, 0:COLS, :] = fluid_ref[3:51, :]
    fbuf[0, COLS:51, :] = fluid_ref[0:3, :] * WAVES
    cbuf[OWN, 0:24, 0:64] = center_ref[3:27, :]
    cbuf[OWN, 0:24, 64:128] = center_ref[27:51, :]
    cbuf[OWN, 24:27, :] = jnp.zeros((3, 128), F32)
    cbuf[OWN, 24:27, 0:64] = center_ref[0:3, :] * WAVES
    fhl[:, 96:128, :] = jnp.zeros((TILES, 32, 256), BF16)

    def poly_column(which):
        return jnp.broadcast_to(poly_ref[which : which + 1, :], (128, COLS)).T

    affine = poly_column(0)
    for axis in range(3):
        affine += poly_column(axis + 1) * fluid_ref[axis : axis + 1, :]
    own[...] = affine

    pl.semaphore_wait(barrier, len(peers))
    started = []

    def start(copy):
        copy.start()
        started.append(copy)
        return copy

    ccopy = {
        k: remote(cbuf.at[OWN], cbuf.at[k], cs.at[k], cr.at[k], plane_dev(*PLANE[k])) for k in OTHERS
    }
    fcopy = [None] * 16
    fcopy[1] = remote(fbuf.at[0], fbuf.at[1], fs.at[1], fr.at[1], sibling)
    for i in range(1, 8):
        fcopy[2 * i] = remote(
            fbuf.at[0], fbuf.at[2 * i], fs.at[2 * i], fr.at[2 * i], line_dev(LINE[i])
        )
        fcopy[2 * i + 1] = remote(
            fbuf.at[2 * i], fbuf.at[2 * i + 1], fs.at[2 * i + 1], fr.at[2 * i + 1], sibling
        )
    for i in range(7):
        start(ccopy[OTHERS[i]])
        start(fcopy[2 * i + 2])
    start(fcopy[1])
    for k in OTHERS[7:]:
        start(ccopy[k])

    def take(n):
        for k in PAIRS[n]:
            if k > 0 and k not in taken:
                taken.append(k)
                fcopy[k].wait_recv()
                if k % 2 == 0:
                    start(fcopy[k + 1])

    taken = []

    low = lax.broadcasted_iota(jnp.int32, (24, 128), 1) < 64

    def turn(value):
        return pltpu.roll(value, 64, 1)

    def unpack_centers(m):
        a, b = cbuf[2 * m], cbuf[2 * m + 1]
        lanes = pl.ds(m * 128, 128)
        coef = jnp.concatenate(
            [jnp.where(low, a[0:24], turn(b[0:24])), jnp.where(low, turn(a[0:24]), b[0:24])], axis=0
        )
        high, rest = split(coef * SCALE)
        chl[0:COLS, lanes] = high
        chl[COLS:96, lanes] = rest
        places = jnp.where(low[0:3], a[24:27], turn(b[24:27]))
        for axis in range(3):
            line = jnp.broadcast_to(places[axis : axis + 1], (128, 128))
            cb[axis, m * 128 : (m + 1) * 128, :] = line.T

    def unpack_fluid(n):
        for part in range(2):
            high, rest = split(fbuf[PAIRS[n][part], 0:COLS, :] * SCALE)
            lanes = pl.ds(part * 128, 128)
            fhl[n, 0:COLS, lanes] = high
            fhl[n, COLS:96, lanes] = rest

    def kernel_tile(half, n, kh, kl):
        places = [[fbuf[k, COLS + axis : COLS + axis + 1, :] for axis in range(3)] for k in PAIRS[n]]
        for first in range(0, HALF, STRIP):
            rows = pl.ds(half * HALF + first, STRIP)
            at = [cb[axis, rows, :] for axis in range(3)]
            for part in range(2):
                dx, dy, dz = (at[axis] - places[part][axis] for axis in range(3))
                sq = dx * dx + dy * dy + dz * dz
                inverse = lax.rsqrt(sq)
                turns = sq * inverse - 0.25
                b = 0.25 - jnp.abs(turns - jnp.round(turns))
                b2 = b * b
                value = b2 + S[3]
                for coefficient in (S[2], S[1], S[0]):
                    value = value * b2 + coefficient
                high, rest = split(value * (b * inverse))
                kh[first : first + STRIP, part * 128 : (part + 1) * 128] = high
                kl[first : first + STRIP, part * 128 : (part + 1) * 128] = rest

    def load_product(half, n, kh, kl):
        forces = fhl[n]
        across = (((1,), (1,)), ((), ()))
        load = lax.dot_general(kh[...], forces, across, preferred_element_type=F32)
        load += lax.dot_general(kl[...], forces, across, preferred_element_type=F32)
        if n == (FIRST if half == 0 else SECOND)[0]:
            lacc[half] = load
        else:
            lacc[half] += load

    def motion_product(half, n, kh, kl):
        coef = chl[:, half * HALF : (half + 1) * HALF]
        motion = jnp.dot(coef, kh[...], preferred_element_type=F32)
        motion += jnp.dot(coef, kl[...], preferred_element_type=F32)
        motion = motion[0:COLS] + motion[COLS:96]
        for part, k in enumerate(PAIRS[n]):
            piece = motion[:, part * 128 : (part + 1) * 128]
            if half == 0:
                macc[k] = piece
            else:
                macc[k] += piece

    def send_loads(half):
        total = lacc[half]
        total = (total + pltpu.roll(total, 80, 1)).T[0:COLS]
        for pair in range(4):
            m = half * 4 + pair
            piece = total[:, pair * 128 : (pair + 1) * 128]
            top, bottom = piece[0:24], piece[24:48]
            lsend[2 * m] = jnp.where(low, top, turn(bottom))
            lsend[2 * m + 1] = jnp.where(low, turn(top), bottom)
        for k in OTHERS:
            if k // 8 == half:
                dx, dy = PLANE[k]
                lcopy[k] = start(
                    remote(lsend.at[k], lrecv.at[k], ls.at[k], lr.at[k], plane_dev(4 - dx, 4 - dy))
                )

    lcopy, scopy, mcopy = {}, {}, {}

    def to_sibling(n):
        for k in PAIRS[n]:
            if k % 2:
                i = k // 2
                scopy[i] = start(remote(macc.at[k], msib.at[i], ss.at[i], sr.at[i], sibling))

    def to_owner(n):
        for k in PAIRS[n]:
            if k % 2 == 0 and k > 0:
                i = k // 2
                scopy[i].wait_recv()
                mout[i] = macc[k] + msib[i]
                mcopy[i] = start(
                    remote(mout.at[i], mrecv.at[i], ms.at[i], mr.at[i], line_dev(8 - LINE[i]))
                )

    buffers = ((kh0, kl0), (kh1, kl1))
    order = [(0, n) for n in FIRST] + [(1, n) for n in SECOND]
    take(0)
    take(1)
    for k in range(8):
        ccopy[k].wait_recv()
    for m in range(4):
        unpack_centers(m)
    for step, (half, n) in enumerate(order):
        if half == 0:
            take(n)
            unpack_fluid(n)
        if step == 5:
            for k in OTHERS[8:]:
                ccopy[k].wait_recv()
            for m in range(4, 8):
                unpack_centers(m)
        kernel_tile(half, n, *buffers[step % 2])
        if step > 0:
            load_product(*order[step - 1], *buffers[(step - 1) % 2])
            motion_product(*order[step - 1], *buffers[(step - 1) % 2])
        if step == TILES:
            send_loads(0)
        if step > TILES:
            to_sibling(order[step - 1][1])
            to_owner(order[step - 1][1])
    load_product(*order[-1], *buffers[(len(order) - 1) % 2])
    send_loads(1)
    motion_product(*order[-1], *buffers[(len(order) - 1) % 2])
    to_owner(0)

    motion = own[...] + macc[0]
    for i in range(1, 8):
        mcopy[i].wait_recv()
        motion += mrecv[i]
    scopy[0].wait_recv()
    motion_ref[...] = motion + msib[0]
    for k in OTHERS:
        lcopy[k].wait_recv()
    load = lsend[OWN]
    for k in OTHERS:
        load += lrecv[k]
    load_ref[0:24, :] = load[:, 0:64]
    load_ref[24:48, :] = load[:, 64:128]
    for copy in started:
        copy.wait_send()


def per_device(fluid_data, center_data, poly_coef):
    vmem = pl.BlockSpec(memory_space=pltpu.VMEM)
    hbm = pl.BlockSpec(memory_space=pltpu.HBM)
    dma = pltpu.SemaphoreType.DMA((16,))
    return pl.pallas_call(
        body,
        out_shape=(
            jax.ShapeDtypeStruct((COLS, 128), F32),
            jax.ShapeDtypeStruct((COLS, 64), F32),
        ),
        in_specs=[hbm] * 3,
        out_specs=(vmem, vmem),
        scratch_shapes=[
            pltpu.VMEM((51, 128), F32),
            pltpu.VMEM((51, 64), F32),
            pltpu.VMEM((4, COLS), F32),
            pltpu.VMEM((16, 51, 128), F32),
            pltpu.VMEM((16, 27, 128), F32),
            pltpu.VMEM((3, 1024, 128), F32),
            pltpu.VMEM((TILES, 128, 256), BF16),
            pltpu.VMEM((96, 1024), BF16),
            pltpu.VMEM((HALF, 256), BF16),
            pltpu.VMEM((HALF, 256), BF16),
            pltpu.VMEM((HALF, 256), BF16),
            pltpu.VMEM((HALF, 256), BF16),
            pltpu.VMEM((2, HALF, 128), F32),
            pltpu.VMEM((16, COLS, 128), F32),
            pltpu.VMEM((8, COLS, 128), F32),
            pltpu.VMEM((8, COLS, 128), F32),
            pltpu.VMEM((8, COLS, 128), F32),
            pltpu.VMEM((16, 24, 128), F32),
            pltpu.VMEM((16, 24, 128), F32),
            pltpu.VMEM((COLS, 128), F32),
            pltpu.SemaphoreType.DMA((3,)),
            *([dma] * 10),
        ],
        compiler_params=pltpu.CompilerParams(
            collective_id=0, has_side_effects=True, vmem_limit_bytes=24 * 2**20
        ),
        name="couple",
    )(
        *(
            pltpu.with_memory_space_constraint(array, pltpu.HBM)
            for array in (fluid_data, center_data, poly_coef.T)
        )
    )


def solution(mesh):
    return jax.shard_map(
        per_device,
        mesh=mesh,
        in_specs=(P(None, ("row", "col")), P(None, ("col", "row")), P()),
        out_specs=(P(None, ("row", "col")), P(None, ("col", "row"))),
        check_vma=False,
    )
```

time: 43.8 us -> 35.5 us (0.81)
  Pallas kernels: 39.5 us -> 33.4 us
  local copies, waits for them, and re-layouts: 3.34 us -> 1.22 us
    pallas_call x1, Pallas kernels: 39.5 us -> 33.4 us  [per_device(): pl.pallas_call(body, out_shape=(jax.ShapeDtypeStruct((COLS, 128), F32), j...]
    unnamed x5 -> x2, local copies, waits for them, and re-layouts: 3.34 us -> 1.22 us
where the time goes in v2:
time: 35.5 us; the launch traced here: 35.2 us
  Pallas kernels  33.4 us (94%)
  local copies, waits for them, and re-layouts  1.22 us (3%)
  between operations  0.64 us (2%)
    pallas_call x1, Pallas kernels, per_device(): pl.pallas_call(body, out_shape=(jax.ShapeDtypeStruct((COLS, 128), F32), j...  33.4 us
    unnamed x2, local copies, waits for them, and re-layouts  1.22 us

profile of v2, /device:TPU:1, one launch (start us, length us, event | category | flops | bytes accessed | tf_op | source)
XLA Modules:
  0.0 35.2 jit_solution(9077675962097340256)
XLA Ops:
  0.6 33.4 %couple.1 = (f32[48,128]{1,0:T(8,128)S(1)}, f32[48,64]{1,0:T(8,128)S(1)}) custom-call(f32[51,128]{1,0:T(8,128)} %fluid_hbm.1, f32[51,64]{1,0:T(8,128)} %center_hbm.1, f32[4,48]{1,0:T(4,128)} %bitcast.1), custom_call_target="tpu_custom_call" | custom-call | tf_op jit(solution)/shard_map/couple/pallas_call | solution.py:281
  34.0 0.6 %copy.7 = f32[48,128]{1,0:T(8,128)} copy(f32[48,128]{1,0:T(8,128)S(1)} %get-tuple-element.4) | data formatting | bytes 49152
  34.6 0.6 %copy.8 = f32[48,64]{1,0:T(8,128)} copy(f32[48,64]{1,0:T(8,128)S(1)} %get-tuple-element.5) | data formatting | bytes 24576

commit v3 on v2

--- a/solution.py
+++ b/solution.py
@@ -16,7 +16,7 @@
 LINE = [0, 1, 7, 2, 6, 3, 5, 4]
 PAIRS = [(0, 2), (4, 6), (8, 10), (12, 14), (1, 3), (5, 7), (9, 11), (13, 15)]
 FIRST = [0, 1, 2, 3, 4, 5, 6, 7]
-SECOND = [7, 6, 5, 3, 4, 2, 1, 0]
+SECOND = [7, 6, 5, 4, 3, 2, 1, 0]
 HALF = 512
 TILES = 8
 STRIP = 32
@@ -234,28 +234,34 @@
         ccopy[k].wait_recv()
     for m in range(4):
         unpack_centers(m)
-    for step, (half, n) in enumerate(order):
-        if half == 0:
-            take(n)
-            unpack_fluid(n)
-        if step == 5:
+    for step in range(0, 16, 2):
+        if step < TILES:
+            for half, n in order[step : step + 2]:
+                take(n)
+                unpack_fluid(n)
+        if step == 4:
             for k in OTHERS[8:]:
                 ccopy[k].wait_recv()
             for m in range(4, 8):
                 unpack_centers(m)
-        kernel_tile(half, n, *buffers[step % 2])
-        if step > 0:
-            load_product(*order[step - 1], *buffers[(step - 1) % 2])
-            motion_product(*order[step - 1], *buffers[(step - 1) % 2])
+        for each in (step, step + 1):
+            kernel_tile(*order[each], *buffers[each % 2])
+            if each > 0:
+                load_product(*order[each - 1], *buffers[(each - 1) % 2])
+                motion_product(*order[each - 1], *buffers[(each - 1) % 2])
         if step == TILES:
             send_loads(0)
-        if step > TILES:
-            to_sibling(order[step - 1][1])
-            to_owner(order[step - 1][1])
+        for each in (step - 1, step):
+            if each >= TILES:
+                to_sibling(order[each][1])
+                to_owner(order[each][1])
     load_product(*order[-1], *buffers[(len(order) - 1) % 2])
     send_loads(1)
     motion_product(*order[-1], *buffers[(len(order) - 1) % 2])
+    early = len(started) - 7
     to_owner(0)
+    for copy in started[:early]:
+        copy.wait_send()
 
     motion = own[...] + macc[0]
     for i in range(1, 8):
@@ -270,20 +276,32 @@
         load += lrecv[k]
     load_ref[0:24, :] = load[:, 0:64]
     load_ref[24:48, :] = load[:, 64:128]
-    for copy in started:
+    for copy in started[early:]:
         copy.wait_send()
+
+
+def deliver(motion_ref, load_ref, motion_out, load_out, sems):
+    copies = [
+        pltpu.make_async_copy(motion_ref, motion_out, sems.at[0]),
+        pltpu.make_async_copy(load_ref, load_out, sems.at[1]),
+    ]
+    for copy in copies:
+        copy.start()
+    for copy in copies:
+        copy.wait()
 
 
 def per_device(fluid_data, center_data, poly_coef):
     vmem = pl.BlockSpec(memory_space=pltpu.VMEM)
     hbm = pl.BlockSpec(memory_space=pltpu.HBM)
     dma = pltpu.SemaphoreType.DMA((16,))
-    return pl.pallas_call(
+    shapes = (
+        jax.ShapeDtypeStruct((COLS, 128), F32),
+        jax.ShapeDtypeStruct((COLS, 64), F32),
+    )
+    outputs = pl.pallas_call(
         body,
-        out_shape=(
-            jax.ShapeDtypeStruct((COLS, 128), F32),
-            jax.ShapeDtypeStruct((COLS, 64), F32),
-        ),
+        out_shape=shapes,
         in_specs=[hbm] * 3,
         out_specs=(vmem, vmem),
         scratch_shapes=[
@@ -320,6 +338,15 @@
             for array in (fluid_data, center_data, poly_coef.T)
         )
     )
+    return pl.pallas_call(
+        deliver,
+        out_shape=shapes,
+        in_specs=[vmem] * 2,
+        out_specs=(hbm, hbm),
+        scratch_shapes=[pltpu.SemaphoreType.DMA((2,))],
+        compiler_params=pltpu.CompilerParams(vmem_limit_bytes=2**20),
+        name="deliver",
+    )(*outputs)
 
 
 def solution(mesh):

time: 35.5 us -> 34.5 us (0.972)
  local copies, waits for them, and re-layouts: 1.22 us -> 0 us
    unnamed x2 -> x0, local copies, waits for them, and re-layouts: 1.22 us -> none
    pallas_call x1 -> x2, Pallas kernels: 33.4 us -> 33.7 us  [the longest x1 33.1 us: per_device(): pl.pallas_call(body, out_shape=shapes, in_specs=[hbm] * 3, out_specs=(vme...]
where the time goes in v3:
time: 34.5 us; the launch traced here: 34.3 us
  Pallas kernels  33.7 us (98%)
  between operations  0.64 us (2%)
    pallas_call x1, Pallas kernels, per_device(): pl.pallas_call(body, out_shape=shapes, in_specs=[hbm] * 3, out_specs=(vme...  33.1 us

profile of v3, /device:TPU:1, one launch (start us, length us, event | category | flops | bytes accessed | tf_op | source)
XLA Modules:
  0.0 34.3 jit_solution(8206975143508278866)
XLA Ops:
  0.6 33.1 %couple.1 = (f32[48,128]{1,0:T(8,128)S(1)}, f32[48,64]{1,0:T(8,128)S(1)}) custom-call(f32[51,128]{1,0:T(8,128)} %fluid_hbm.1, f32[51,64]{1,0:T(8,128)} %center_hbm.1, f32[4,48]{1,0:T(4,128)} %bitcast.1), custom_call_target="tpu_custom_call" | custom-call | tf_op jit(solution)/shard_map/couple/pallas_call | solution.py:302
  33.7 0.6 %deliver.1 = (f32[48,128]{1,0:T(8,128)}, f32[48,64]{1,0:T(8,128)}) custom-call(f32[48,128]{1,0:T(8,128)S(1)} %get-tuple-element.4.motion_ref, f32[48,64]{1,0:T(8,128)S(1)} %get-tuple-element.5.load_ref), custom_call_target="tpu_custom_call" | custom-call | tf_op jit(solution)/shard_map/deliver/pallas_call | solution.py:341

commit v4 on v3

--- a/solution.py
+++ b/solution.py
@@ -108,10 +108,10 @@
         fcopy[2 * i + 1] = remote(
             fbuf.at[2 * i], fbuf.at[2 * i + 1], fs.at[2 * i + 1], fr.at[2 * i + 1], sibling
         )
+    start(fcopy[1])
     for i in range(7):
         start(ccopy[OTHERS[i]])
         start(fcopy[2 * i + 2])
-    start(fcopy[1])
     for k in OTHERS[7:]:
         start(ccopy[k])
 
@@ -229,7 +229,6 @@
     buffers = ((kh0, kl0), (kh1, kl1))
     order = [(0, n) for n in FIRST] + [(1, n) for n in SECOND]
     take(0)
-    take(1)
     for k in range(8):
         ccopy[k].wait_recv()
     for m in range(4):
@@ -249,7 +248,7 @@
             if each > 0:
                 load_product(*order[each - 1], *buffers[(each - 1) % 2])
                 motion_product(*order[each - 1], *buffers[(each - 1) % 2])
-        if step == TILES:
+        if step == TILES + 4:
             send_loads(0)
         for each in (step - 1, step):
             if each >= TILES:

time: 34.5 us -> 34.2 us (level)
  no operation moved by 1% of the time
where the time goes in v4:
time: 34.2 us; the launch traced here: 34 us
  Pallas kernels  33.4 us (98%)
  between operations  0.64 us (2%)
    pallas_call x1, Pallas kernels, per_device(): pl.pallas_call(body, out_shape=shapes, in_specs=[hbm] * 3, out_specs=(vme...  32.7 us

profile of v4, /device:TPU:1, one launch (start us, length us, event | category | flops | bytes accessed | tf_op | source)
XLA Modules:
  0.0 34.0 jit_solution(4812970252477989485)
XLA Ops:
  0.6 32.7 %couple.1 = (f32[48,128]{1,0:T(8,128)S(1)}, f32[48,64]{1,0:T(8,128)S(1)}) custom-call(f32[51,128]{1,0:T(8,128)} %fluid_hbm.1, f32[51,64]{1,0:T(8,128)} %center_hbm.1, f32[4,48]{1,0:T(4,128)} %bitcast.1), custom_call_target="tpu_custom_call" | custom-call | tf_op jit(solution)/shard_map/couple/pallas_call | solution.py:301
  33.4 0.6 %deliver.1 = (f32[48,128]{1,0:T(8,128)}, f32[48,64]{1,0:T(8,128)}) custom-call(f32[48,128]{1,0:T(8,128)S(1)} %get-tuple-element.4.motion_ref, f32[48,64]{1,0:T(8,128)S(1)} %get-tuple-element.5.load_ref), custom_call_target="tpu_custom_call" | custom-call | tf_op jit(solution)/shard_map/deliver/pallas_call | solution.py:340

commit v5 on v4

--- a/solution.py
+++ b/solution.py
@@ -64,8 +64,8 @@
         copy.start()
     sibling = line_dev(0, 1)
     barrier = pltpu.get_barrier_semaphore()
-    peers = [plane_dev(*PLANE[k]) for k in OTHERS]
-    peers += [line_dev(LINE[i]) for i in range(1, 8)] + [sibling]
+    peers = [line_dev(LINE[i]) for i in reversed(range(1, 8))]
+    peers += [plane_dev(*PLANE[k]) for k in OTHERS] + [sibling]
     for dev in peers:
         pl.semaphore_signal(barrier, inc=1, device_id=dev, device_id_type=pl.DeviceIdType.MESH)
 

time: 34.2 us -> 34.1 us (level)
  Pallas kernels: 33.4 us -> 33 us
    pallas_call x1, Pallas kernels: 32.7 us -> 32.4 us  [per_device(): pl.pallas_call(body, out_shape=shapes, in_specs=[hbm] * 3, out_specs=(vme...]
where the time goes in v5:
time: 34.1 us; the launch traced here: 33.7 us
  Pallas kernels  33 us (97%)
  between operations  0.64 us (2%)
    pallas_call x1, Pallas kernels, per_device(): pl.pallas_call(body, out_shape=shapes, in_specs=[hbm] * 3, out_specs=(vme...  32.4 us

profile of v5, /device:TPU:1, one launch (start us, length us, event | category | flops | bytes accessed | tf_op | source)
XLA Modules:
  0.0 33.7 jit_solution(10032802594736900935)
XLA Ops:
  0.6 32.4 %couple.1 = (f32[48,128]{1,0:T(8,128)S(1)}, f32[48,64]{1,0:T(8,128)S(1)}) custom-call(f32[51,128]{1,0:T(8,128)} %fluid_hbm.1, f32[51,64]{1,0:T(8,128)} %center_hbm.1, f32[4,48]{1,0:T(4,128)} %bitcast.1), custom_call_target="tpu_custom_call" | custom-call | tf_op jit(solution)/shard_map/couple/pallas_call | solution.py:301
  33.0 0.6 %deliver.1 = (f32[48,128]{1,0:T(8,128)}, f32[48,64]{1,0:T(8,128)}) custom-call(f32[48,128]{1,0:T(8,128)S(1)} %get-tuple-element.4.motion_ref, f32[48,64]{1,0:T(8,128)S(1)} %get-tuple-element.5.load_ref), custom_call_target="tpu_custom_call" | custom-call | tf_op jit(solution)/shard_map/deliver/pallas_call | solution.py:340
